TPU v7x, 32 devices: a whole 2x2x4 slice. The times are simulated.
32 devices in a mesh: dp: 8 (over y, x, core), tensor: 4 (over z).
Axes of the slice: x: 2, y: 2, z: 4, core: 2. Of those that a mesh axis runs over, the one named last changes fastest.
Arguments:
- hidden_in: float32 [8192, 2048], P(('dp', 'tensor')), may hold values from -6 to 6
- positions: int32 [8192], P('dp'), may hold values from 0 to 4095
- norm_gains: bfloat16 [1, 2, 2048], P(None, None, ('dp', 'tensor')), may hold values from 0.25 to 1.75
- w_query: bfloat16 [1, 2048, 2048], P(None, 'dp', 'tensor'), may hold values from -0.125 to 0.125
- w_key: bfloat16 [1, 2048, 256], P(None, ('dp', 'tensor')), may hold values from -0.125 to 0.125
- w_value: bfloat16 [1, 2048, 256], P(None, ('dp', 'tensor')), may hold values from -0.125 to 0.125
- w_out: bfloat16 [1, 2048, 2048], P(None, 'tensor', 'dp'), may hold values from -0.5 to 0.5
- w_gate: bfloat16 [1, 2048, 5632], P(None, 'dp', 'tensor'), may hold values from -0.125 to 0.125
- w_up: bfloat16 [1, 2048, 5632], P(None, 'dp', 'tensor'), may hold values from -0.125 to 0.125
- w_down: bfloat16 [1, 5632, 2048], P(None, 'tensor', 'dp'), may hold values from -0.078125 to 0.078125
- out_grad: float32 [8192, 2048], P(('dp', 'tensor')), may hold values from -6 to 6
Outputs:
- hidden_out: float32 [8192, 2048], P(('dp', 'tensor'))
- grad_in: float32 [8192, 2048], P(('dp', 'tensor'))
- grad_gains: float32 [1, 2, 2048], P(None, None, ('dp', 'tensor'))
- grad_query: float32 [1, 2048, 2048], P(None, 'dp', 'tensor')
- grad_key: float32 [1, 2048, 256], P(None, ('dp', 'tensor'))
- grad_value: float32 [1, 2048, 256], P(None, ('dp', 'tensor'))
- grad_out: float32 [1, 2048, 2048], P(None, 'tensor', 'dp')
- grad_gate: float32 [1, 2048, 5632], P(None, 'dp', 'tensor')
- grad_up: float32 [1, 2048, 5632], P(None, 'dp', 'tensor')
- grad_down: float32 [1, 5632, 2048], P(None, 'tensor', 'dp')
All inputs are finite; a program needn't handle non-finite values.
Results may differ from a plain program's by a relative error of at most 0.019.
Values may be sent and summed in bfloat16 or wider, within the bound.
A program may use at most 192 MiB of HBM per device.

v0:
```python
import jax
import jax.numpy as jnp
from jax import lax
from jax.sharding import PartitionSpec as P

D = 2048
H = 32
KV = 4
HD = 64
SEQ = 128
NORM_EPS = 1e-05
NEG_BIG = -1e30


def rms_normed(row_vals, gain_vec):
    inv_rms = lax.rsqrt(jnp.mean(row_vals * row_vals, -1, keepdims=True) + NORM_EPS)
    return (row_vals * inv_rms * gain_vec.astype(jnp.float32)).astype(jnp.bfloat16)


def rms_back(row_vals, gain_vec, grad_normed):
    inv_rms = lax.rsqrt(jnp.mean(row_vals * row_vals, -1, keepdims=True) + NORM_EPS)
    weighted = grad_normed * gain_vec.astype(jnp.float32)
    grad_gain = jnp.sum(grad_normed * row_vals * inv_rms, 0)
    grad_rows = inv_rms * weighted - row_vals * inv_rms**3 * jnp.mean(
        weighted * row_vals, -1, keepdims=True
    )
    return (grad_rows, grad_gain)


def rope_tables(positions):
    inv_freq = 10000.0 ** (-(jnp.arange(HD // 2, dtype=jnp.float32) * 2.0 / HD))
    angles = positions.astype(jnp.float32)[:, None] * inv_freq[None, :]
    return (jnp.cos(angles), jnp.sin(angles))


def rotate(row_vals, cosine_tab, sine_tab):
    row_total = row_vals.shape[0]
    shaped = row_vals.reshape(row_total, -1, HD)
    front_half = shaped[..., : HD // 2]
    back_half = shaped[..., HD // 2 :]
    cos_part = cosine_tab[:, None, :]
    sin_part = sine_tab[:, None, :]
    turned = jnp.concatenate(
        [
            front_half * cos_part - back_half * sin_part,
            back_half * cos_part + front_half * sin_part,
        ],
        -1,
    )
    return turned.reshape(row_total, -1)


def rotate_back(row_vals, cosine_tab, sine_tab):
    row_total = row_vals.shape[0]
    shaped = row_vals.reshape(row_total, -1, HD)
    front_half = shaped[..., : HD // 2]
    back_half = shaped[..., HD // 2 :]
    cos_part = cosine_tab[:, None, :]
    sin_part = sine_tab[:, None, :]
    turned = jnp.concatenate(
        [
            front_half * cos_part + back_half * sin_part,
            back_half * cos_part - front_half * sin_part,
        ],
        -1,
    )
    return turned.reshape(row_total, -1)


def head_major(values_in, seq_len):
    head_count = values_in.shape[1] // HD
    return (
        values_in.reshape(seq_len, head_count, HD)
        .transpose(1, 0, 2)
        .reshape(head_count * seq_len, HD)
    )


def seq_major(values_in, seq_len):
    head_count = values_in.shape[0] // seq_len
    return (
        values_in.reshape(head_count, seq_len, HD)
        .transpose(1, 0, 2)
        .reshape(seq_len, head_count * HD)
    )


def causal_scores(query_rows, key_rows):
    seq_len = key_rows.shape[0]
    scores = jnp.dot(query_rows, key_rows.T, preferred_element_type=jnp.float32) * HD ** (-0.5)
    row_pos = lax.broadcasted_iota(jnp.int32, scores.shape, 0) % seq_len
    col_pos = lax.broadcasted_iota(jnp.int32, scores.shape, 1)
    return jnp.where(col_pos <= row_pos, scores, NEG_BIG)


def attend_forward(query_rows, key_rows, value_rows):
    scores = causal_scores(query_rows, key_rows)
    row_max = jnp.max(scores, -1, keepdims=True)
    log_total = row_max[:, 0] + jnp.log(jnp.sum(jnp.exp(scores - row_max), -1))
    attn_prob = jnp.exp(scores - log_total[:, None]).astype(jnp.bfloat16)
    return (jnp.dot(attn_prob, value_rows, preferred_element_type=jnp.float32), log_total)


def attend_backward(query_rows, key_rows, value_rows, log_total, grad_rows):
    seq_len = key_rows.shape[0]
    head_count = query_rows.shape[0] // seq_len
    scores = causal_scores(query_rows, key_rows)
    attn_prob = jnp.exp(scores - log_total[:, None])
    prob_bf = attn_prob.astype(jnp.bfloat16)
    grad_prob = jnp.dot(grad_rows, value_rows.T, preferred_element_type=jnp.float32)
    delta = jnp.sum(attn_prob * grad_prob, -1, keepdims=True)
    grad_scores = (attn_prob * (grad_prob - delta) * HD ** (-0.5)).astype(jnp.bfloat16)
    grad_query = jnp.dot(grad_scores, key_rows, preferred_element_type=jnp.float32)
    scores_3d = grad_scores.reshape(head_count, seq_len, seq_len)
    query_3d = query_rows.reshape(head_count, seq_len, HD)
    prob_3d = prob_bf.reshape(head_count, seq_len, seq_len)
    grad_3d = grad_rows.reshape(head_count, seq_len, HD)
    grad_key = jnp.einsum("hqk,hqd->hkd", scores_3d, query_3d, preferred_element_type=jnp.float32)
    grad_value = jnp.einsum("hqk,hqd->hkd", prob_3d, grad_3d, preferred_element_type=jnp.float32)
    return (
        grad_query,
        grad_key.reshape(head_count * seq_len, HD),
        grad_value.reshape(head_count * seq_len, HD),
    )


def tdot(left_op, right_op):
    return lax.dot_general(
        left_op, right_op, (((0,), (0,)), ((), ())), preferred_element_type=jnp.float32
    )


def fetch_weights(layer_index, w_query, w_key, w_value, w_out, w_gate, w_up, w_down, norm_gains):
    large = (
        lax.all_gather(w_query[layer_index], "dp", axis=0, tiled=True),
        lax.all_gather(w_out[layer_index], "dp", axis=1, tiled=True),
        lax.all_gather(w_gate[layer_index], "dp", axis=0, tiled=True),
        lax.all_gather(w_up[layer_index], "dp", axis=0, tiled=True),
        lax.all_gather(w_down[layer_index], "dp", axis=1, tiled=True),
    )
    small = (
        lax.all_gather(w_key[layer_index], ("dp", "tensor"), axis=0, tiled=True),
        lax.all_gather(w_value[layer_index], ("dp", "tensor"), axis=0, tiled=True),
        lax.all_gather(norm_gains[layer_index], ("dp", "tensor"), axis=1, tiled=True),
    )
    return tuple(large) + tuple(small)


def gather_rows(row_vals):
    return lax.all_gather(row_vals, "tensor", axis=0, tiled=True)


def sum_rows(term, rows_dev):
    return lax.psum_scatter(
        term(jnp.int32(0), rows_dev * lax.axis_size("tensor")),
        "tensor",
        scatter_dimension=0,
        tiled=True,
    )


def on_device(
    hidden_in, positions, norm_gains, w_query, w_key, w_value, w_out, w_gate, w_up, w_down, out_grad
):
    rows_dev = hidden_in.shape[0]
    block_rows = positions.shape[0]
    seq_count = block_rows // SEQ
    layers = w_query.shape[0]
    heads_dev = w_query.shape[2] // HD
    kv_head = lax.axis_index("tensor") * heads_dev // (H // KV)
    cosine_tab, sine_tab = rope_tables(positions)

    def pick_head(weight_kv):
        return lax.dynamic_slice_in_dim(weight_kv, kv_head * HD, HD, 1)

    def by_sequence(values_in):
        return values_in.reshape(seq_count, SEQ, -1)

    def one_forward(pieces):
        query_seq, key_seq, value_seq = pieces
        attended, log_total = attend_forward(head_major(query_seq, SEQ), key_seq, value_seq)
        return (seq_major(attended, SEQ).astype(jnp.bfloat16), log_total)

    def one_backward(pieces):
        query_seq, key_seq, value_seq, log_seq, grad_seq = pieces
        grad_query, grad_key, grad_value = attend_backward(
            head_major(query_seq, SEQ), key_seq, value_seq, log_seq, head_major(grad_seq, SEQ)
        )
        return (seq_major(grad_query, SEQ), seq_major(grad_key, SEQ), seq_major(grad_value, SEQ))

    layer_index = 0
    weights = fetch_weights(
        layer_index, w_query, w_key, w_value, w_out, w_gate, w_up, w_down, norm_gains
    )
    wq, wo, wg, wu, wd, wk_all, wv_all, gain_pair = weights
    wk = pick_head(wk_all)
    wv = pick_head(wv_all)
    normed_one = gather_rows(rms_normed(hidden_in, gain_pair[0]))
    query_all = rotate(
        jnp.dot(normed_one, wq, preferred_element_type=jnp.float32), cosine_tab, sine_tab
    ).astype(jnp.bfloat16)
    key_all = rotate(
        jnp.dot(normed_one, wk, preferred_element_type=jnp.float32), cosine_tab, sine_tab
    ).astype(jnp.bfloat16)
    value_all = jnp.dot(normed_one, wv, preferred_element_type=jnp.float32).astype(jnp.bfloat16)
    attended, log_total = lax.map(
        one_forward, (by_sequence(query_all), by_sequence(key_all), by_sequence(value_all))
    )
    attended = attended.reshape(block_rows, -1)
    middle = hidden_in + sum_rows(
        lambda offset, length: jnp.dot(attended, wo, preferred_element_type=jnp.float32), rows_dev
    )
    normed_two = gather_rows(rms_normed(middle, gain_pair[1]))
    gate_pre = jnp.dot(normed_two, wg, preferred_element_type=jnp.float32)
    up_pre = jnp.dot(normed_two, wu, preferred_element_type=jnp.float32)
    hidden = (gate_pre * jax.nn.sigmoid(gate_pre) * up_pre).astype(jnp.bfloat16)
    output = middle + sum_rows(
        lambda offset, length: jnp.dot(hidden, wd, preferred_element_type=jnp.float32), rows_dev
    )
    saved = [
        (
            hidden_in,
            normed_one,
            query_all,
            key_all,
            value_all,
            attended,
            log_total,
            middle,
            normed_two,
            gate_pre,
            up_pre,
            hidden,
        )
    ]
    cotangent = out_grad
    layer_grads = [None] * layers
    for layer_index in reversed(range(layers)):
        weights = fetch_weights(
            layer_index, w_query, w_key, w_value, w_out, w_gate, w_up, w_down, norm_gains
        )
        wq, wo, wg, wu, wd, wk_all, wv_all, gain_pair = weights
        wk = pick_head(wk_all)
        wv = pick_head(wv_all)
        (
            layer_in,
            normed_one,
            query_all,
            key_all,
            value_all,
            attended,
            log_total,
            middle,
            normed_two,
            gate_pre,
            up_pre,
            hidden,
        ) = saved[layer_index]
        top_all = gather_rows(cotangent.astype(jnp.bfloat16))
        grad_down = tdot(hidden, top_all)
        grad_hidden = jnp.dot(top_all, wd.T, preferred_element_type=jnp.float32)
        sigmoid_gate = jax.nn.sigmoid(gate_pre)
        grad_gate_pre = (
            grad_hidden * up_pre * sigmoid_gate * (1.0 + gate_pre * (1.0 - sigmoid_gate))
        ).astype(jnp.bfloat16)
        grad_up_pre = (grad_hidden * gate_pre * sigmoid_gate).astype(jnp.bfloat16)
        grad_gate = tdot(normed_two, grad_gate_pre)
        grad_up = tdot(normed_two, grad_up_pre)
        grad_normed_two = sum_rows(
            lambda offset, length: jnp.dot(grad_gate_pre, wg.T, preferred_element_type=jnp.float32)
            + jnp.dot(grad_up_pre, wu.T, preferred_element_type=jnp.float32),
            rows_dev,
        )
        grad_mid_norm, grad_gain_two = rms_back(middle, gain_pair[1], grad_normed_two)
        grad_middle = cotangent + grad_mid_norm
        middle_all = gather_rows(grad_middle.astype(jnp.bfloat16))
        grad_out = tdot(attended, middle_all)
        grad_attended = jnp.dot(middle_all, wo.T, preferred_element_type=jnp.float32).astype(
            jnp.bfloat16
        )
        grads = lax.map(
            one_backward,
            (
                by_sequence(query_all),
                by_sequence(key_all),
                by_sequence(value_all),
                log_total,
                by_sequence(grad_attended),
            ),
        )
        grad_q = rotate_back(grads[0].reshape(block_rows, -1), cosine_tab, sine_tab).astype(
            jnp.bfloat16
        )
        grad_k = rotate_back(grads[1].reshape(block_rows, -1), cosine_tab, sine_tab).astype(
            jnp.bfloat16
        )
        grad_v = grads[2].reshape(block_rows, -1).astype(jnp.bfloat16)
        grad_query = tdot(normed_one, grad_q)
        key_local = jnp.sum(tdot(normed_one, grad_k).reshape(D, heads_dev, HD), 1)
        value_local = jnp.sum(tdot(normed_one, grad_v).reshape(D, heads_dev, HD), 1)
        wk_tiled = jnp.tile(wk, (1, heads_dev))
        wv_tiled = jnp.tile(wv, (1, heads_dev))
        grad_normed_one = sum_rows(
            lambda offset, length: jnp.dot(grad_q, wq.T, preferred_element_type=jnp.float32)
            + jnp.dot(grad_k, wk_tiled.T, preferred_element_type=jnp.float32)
            + jnp.dot(grad_v, wv_tiled.T, preferred_element_type=jnp.float32),
            rows_dev,
        )
        grad_in_norm, grad_gain_one = rms_back(layer_in, gain_pair[0], grad_normed_one)
        cotangent = grad_middle + grad_in_norm
        zero_heads = jnp.zeros((D, KV * HD), jnp.float32)
        grad_key = lax.dynamic_update_slice_in_dim(zero_heads, key_local, kv_head * HD, 1)
        grad_value = lax.dynamic_update_slice_in_dim(zero_heads, value_local, kv_head * HD, 1)
        grad_gain_pair = jnp.stack([grad_gain_one, grad_gain_two])
        large_grads = tuple(
            (
                lax.psum_scatter(
                    grad_query.astype(jnp.bfloat16), "dp", scatter_dimension=0, tiled=True
                ).astype(jnp.float32),
                lax.psum_scatter(
                    grad_out.astype(jnp.bfloat16), "dp", scatter_dimension=1, tiled=True
                ).astype(jnp.float32),
                lax.psum_scatter(
                    grad_gate.astype(jnp.bfloat16), "dp", scatter_dimension=0, tiled=True
                ).astype(jnp.float32),
                lax.psum_scatter(
                    grad_up.astype(jnp.bfloat16), "dp", scatter_dimension=0, tiled=True
                ).astype(jnp.float32),
                lax.psum_scatter(
                    grad_down.astype(jnp.bfloat16), "dp", scatter_dimension=1, tiled=True
                ).astype(jnp.float32),
            )
        )
        small_grads = tuple(
            (
                lax.psum_scatter(grad_key, ("dp", "tensor"), scatter_dimension=0, tiled=True),
                lax.psum_scatter(grad_value, ("dp", "tensor"), scatter_dimension=0, tiled=True),
                lax.psum_scatter(grad_gain_pair, ("dp", "tensor"), scatter_dimension=1, tiled=True),
            )
        )
        layer_grads[layer_index] = large_grads + small_grads
    stacked = [jnp.stack([layer_grads[0][kind]]) for kind in range(8)]
    return (
        output,
        cotangent,
        stacked[7],
        stacked[0],
        stacked[5],
        stacked[6],
        stacked[1],
        stacked[2],
        stacked[3],
        stacked[4],
    )


def solution(mesh):
    placed = (
        P(("dp", "tensor"), None),
        P("dp"),
        P(None, None, ("dp", "tensor")),
        P(None, "dp", "tensor"),
        P(None, ("dp", "tensor"), None),
        P(None, ("dp", "tensor"), None),
        P(None, "tensor", "dp"),
        P(None, "dp", "tensor"),
        P(None, "dp", "tensor"),
        P(None, "tensor", "dp"),
        P(("dp", "tensor"), None),
    )
    return jax.shard_map(
        on_device,
        mesh=mesh,
        in_specs=placed,
        out_specs=(
            P(("dp", "tensor"), None),
            P(("dp", "tensor"), None),
            P(None, None, ("dp", "tensor")),
            P(None, "dp", "tensor"),
            P(None, ("dp", "tensor"), None),
            P(None, ("dp", "tensor"), None),
            P(None, "tensor", "dp"),
            P(None, "dp", "tensor"),
            P(None, "dp", "tensor"),
            P(None, "tensor", "dp"),
        ),
        check_vma=False,
    )
```

profile of v0, /device:TPU:0, one launch (start us, length us, event | category | flops | bytes accessed | tf_op | source)
XLA Modules:
  0.0 2196.6 jit_solution(15463837602519331557)
XLA Ops:
  9.5 79.8 %all-gather = bf16[1,2,2048]{1,0,2:T(2,128)(2,1)S(1)} all-gather(bf16[1,2,64]{1,0,2:T(2,128)(2,1)S(1)} %copy.87), channel_id=2, replica_groups=mesh['dp'=8,'tensor'=4] {'dp','tensor'}, dimensions={2}, use_global_device_ids=true | all-gather | bytes 8448 | tf_op jit(solution)/shard_map/all_gather | solution.py:144
  91.7 33.5 %fusion.68 = (f32[2048]{0:T(1024)S(1)}, f32[2048]{0:T(1024)S(1)}) fusion(bf16[1,2,2048]{1,0,2:T(2,128)(2,1)S(1)} %all-gather), kind=kLoop, calls=%fused_computation.104 | loop fusion | flops 4096 | bytes 24576 | tf_op jit(solution)/shard_map/mul | solution.py:17
  131.0 75.3 %all-gather.20.cloned.1.call-done = bf16[1024,2048]{1,0:T(8,128)(2,1)} async-done(((bf16[256,2048]{1,0:T(8,128)(2,1)}), bf16[1024,2048]{1,0:T(8,128)(2,1)}) %all-gather.20.cloned.1.call-update) | async-done | bytes 4194320 | tf_op jit(solution)/shard_map/all_gather | solution.py:150
  213.4 20.9 all-gather.28.cloned.1.call-done
  240.5 49.7 %while.30 = (s32[]{:T(128)}, bf16[8,128,512]{2,1,0:T(8,128)(2,1)}, f32[8,1024]{1,0:T(8,128)}, bf16[8,128,512]{1,2,0:T(8,128)(2,1)S(1)}, bf16[8,128,64]{1,0,2:T(8...) while((s32[]{:T(128)}, bf16[8,128,512]{2,1,0:T(8,128)(2,1)}, f32[8,1024]{1,0:T(8,128)}, ...), condition=%wide.region_4.5_spmd, body=%wide.region_1.4_spmd.sunk | while | flops 34804736 | bytes 3300449 | solution.py:206
  302.1 140.4 %reduce-scatter.15.cloned.1.call-done = f32[256,2048]{1,0:T(8,128)} async-done(((f32[1024,2048]{1,0:T(8,128)}), f32[256,2048]{1,0:T(8,128)}) %reduce-scatter.15.cloned.1.call-update) | async-done | bytes 2097168 | tf_op jit(solution)/shard_map/reduce_scatter | solution.py:154
  447.9 78.1 %all-gather.24.cloned.1.call-done = bf16[1024,2048]{1,0:T(8,128)(2,1)} async-done(((bf16[256,2048]{1,0:T(8,128)(2,1)}), bf16[1024,2048]{1,0:T(8,128)(2,1)}) %all-gather.24.cloned.1.call-update) | async-done | bytes 4194320 | tf_op jit(solution)/shard_map/all_gather | solution.py:150
  526.0 44.7 %all-gather.40.cloned.1.call-done = bf16[1,1408,2048]{2,1,0:T(8,128)(2,1)} async-done(((bf16[1,1408,256]{2,1,0:T(8,128)(2,1)}), bf16[1,1408,2048]{2,1,0:T(8,128)(2,1)}) %all-gather.40.cloned.1.call-update) | async-done | bytes 5767184 | tf_op jit(solution)/shard_map/all_gather | solution.py:139
  570.7 11.7 fusion.32
  582.4 33.4 %all-gather.38.cloned.1.call-done = bf16[1,2048,1408]{2,1,0:T(8,128)(2,1)} async-done(((bf16[1,256,1408]{2,1,0:T(8,128)(2,1)}), bf16[1,2048,1408]{2,1,0:T(8,128)(2,1)}) %all-gather.38.cloned.1.call-update) | async-done | bytes 5767184 | tf_op jit(solution)/shard_map/all_gather | solution.py:138
  615.8 82.8 %all-gather.22.cloned.1.call-done = bf16[1024,2048]{1,0:T(8,128)(2,1)} async-done(((bf16[256,2048]{1,0:T(8,128)(2,1)}), bf16[1024,2048]{1,0:T(8,128)(2,1)}) %all-gather.22.cloned.1.call-update) | async-done | bytes 4194320 | tf_op jit(solution)/shard_map/all_gather | solution.py:150
  698.6 11.7 fusion.38
  710.2 31.9 %all-gather.36.cloned.1.call-done = bf16[1,2048,1408]{2,1,0:T(8,128)(2,1)} async-done(((bf16[1,256,1408]{2,1,0:T(8,128)(2,1)}), bf16[1,2048,1408]{2,1,0:T(8,128)(2,1)}) %all-gather.36.cloned.1.call-update) | async-done | bytes 5767184 | tf_op jit(solution)/shard_map/all_gather | solution.py:137
  742.2 16.1 multiply_convert_fusion.2
  758.2 9.0 fusion.36
  767.3 11.0 fusion.48
  778.7 11.6 fusion.34
  790.4 132.6 %reduce-scatter.19.cloned.1.call-done = f32[256,2048]{1,0:T(8,128)} async-done(((f32[1024,2048]{1,0:T(8,128)}), f32[256,2048]{1,0:T(8,128)}) %reduce-scatter.19.cloned.1.call-update) | async-done | bytes 2097168 | tf_op jit(solution)/shard_map/reduce_scatter | solution.py:154
  925.8 144.9 %reduce-scatter.17.cloned.1.call-done = f32[256,2048]{1,0:T(8,128)} async-done(((f32[1024,2048]{1,0:T(8,128)}), f32[256,2048]{1,0:T(8,128)}) %reduce-scatter.17.cloned.1.call-update) | async-done | bytes 2097168 | tf_op jit(solution)/shard_map/reduce_scatter | solution.py:154
  1081.3 76.8 %all-gather.26.cloned.1.call-done = bf16[1024,2048]{1,0:T(8,128)(2,1)} async-done(((bf16[256,2048]{1,0:T(8,128)(2,1)}), bf16[1024,2048]{1,0:T(8,128)(2,1)}) %all-gather.26.cloned.1.call-update) | async-done | bytes 4194320 | tf_op jit(solution)/shard_map/all_gather | solution.py:150
  1163.4 171.1 %while.31 = (s32[]{:T(128)}, f32[8,128,512]{1,0,2:T(8,128)}, f32[8,128,512]{1,0,2:T(8,128)}, bf16[8,128,512]{2,1,0:T(8,128)(2,1)}, bf16[8,128,512]{1,2,0:T(8,128...) while((s32[]{:T(128)}, f32[8,128,512]{1,0,2:T(8,128)}, ...), condition=%wide.region_12.13_spmd, body=%wide.region_10.12_spmd.sunk | while | flops 85464064 | bytes 7626373 | solution.py:281
  1166.8 8.0 dynamic_update_slice.52
  1175.7 8.0 dynamic_update_slice.51
  1188.2 8.0 dynamic_update_slice.52
  1197.1 8.0 dynamic_update_slice.51
  1209.5 8.0 dynamic_update_slice.52
  1218.5 8.0 dynamic_update_slice.51
  1230.9 8.0 dynamic_update_slice.52
  1239.9 8.0 dynamic_update_slice.51
  1252.3 8.0 dynamic_update_slice.52
  1261.3 8.0 dynamic_update_slice.51
  1273.7 8.0 dynamic_update_slice.52
  1282.7 8.0 dynamic_update_slice.51
  1295.1 8.0 dynamic_update_slice.52
  1316.5 8.0 dynamic_update_slice.52
  1325.5 8.0 dynamic_update_slice.51
  1351.3 11.2 convolution_convert_fusion.2
  1362.6 11.0 convolution_convert_fusion.3
  1373.6 10.5 convolution_convert_fusion.1
  1396.6 98.0 %reduce-scatter.21.cloned.1.call-done = f32[256,2048]{1,0:T(8,128)} async-done(((f32[1024,2048]{1,0:T(8,128)}), f32[256,2048]{1,0:T(8,128)}) %reduce-scatter.21.cloned.1.call-update) | async-done | bytes 2097168 | tf_op jit(solution)/shard_map/reduce_scatter | solution.py:154
  1528.2 29.4 %reduce-scatter.33.cloned.1.call-done = bf16[256,1408]{1,0:T(8,128)(2,1)} async-done(((bf16[2048,1408]{1,0:T(8,128)(2,1)}), bf16[256,1408]{1,0:T(8,128)(2,1)}) %reduce-scatter.33.cloned.1.call-update) | async-done | bytes 720912 | tf_op jit(solution)/shard_map/reduce_scatter | solution.py:326
  1559.8 60.0 %reduce-scatter.31.cloned.1.call-done = bf16[256,1408]{1,0:T(8,128)(2,1)} async-done(((bf16[2048,1408]{1,0:T(8,128)(2,1)}), bf16[256,1408]{1,0:T(8,128)(2,1)}) %reduce-scatter.31.cloned.1.call-update) | async-done | bytes 720912 | tf_op jit(solution)/shard_map/reduce_scatter | solution.py:323
  1622.2 59.9 %reduce-scatter.35.cloned.1.call-done = bf16[1408,256]{1,0:T(8,128)(2,1)} async-done(((bf16[1408,2048]{1,0:T(8,128)(2,1)}), bf16[1408,256]{1,0:T(8,128)(2,1)}) %reduce-scatter.35.cloned.1.call-update) | async-done | bytes 720912 | tf_op jit(solution)/shard_map/reduce_scatter | solution.py:329
  1684.4 42.1 %reduce-scatter.23.cloned.1.call-done = bf16[256,512]{1,0:T(8,128)(2,1)} async-done(((bf16[2048,512]{1,0:T(8,128)(2,1)}), bf16[256,512]{1,0:T(8,128)(2,1)}) %reduce-scatter.23.cloned.1.call-update) | async-done | bytes 262160 | tf_op jit(solution)/shard_map/reduce_scatter | solution.py:317
  1728.3 42.5 %reduce-scatter.29.cloned.1.call-done = bf16[512,256]{1,0:T(8,128)(2,1)} async-done(((bf16[512,2048]{1,0:T(8,128)(2,1)}), bf16[512,256]{1,0:T(8,128)(2,1)}) %reduce-scatter.29.cloned.1.call-update) | async-done | bytes 262160 | tf_op jit(solution)/shard_map/reduce_scatter | solution.py:320
  1776.6 133.5 %reduce-scatter.37.cloned.1.call-done = f32[64,2]{1,0:T(8,128)} async-done(((f32[2048,2]{1,0:T(8,128)}), f32[64,2]{1,0:T(8,128)}) %reduce-scatter.37.cloned.1.call-update) | async-done | bytes 528
  1911.5 138.2 %reduce-scatter.25.cloned.1.call-done = f32[64,256]{1,0:T(8,128)} async-done(((f32[2048,256]{1,0:T(8,128)}), f32[64,256]{1,0:T(8,128)}) %reduce-scatter.25.cloned.1.call-update) | async-done | bytes 65552 | tf_op jit(solution)/shard_map/reduce_scatter | solution.py:336
  2049.7 140.2 %reduce-scatter.27.cloned.1.call-done = f32[64,256]{1,0:T(8,128)} async-done(((f32[2048,256]{1,0:T(8,128)}), f32[64,256]{1,0:T(8,128)}) %reduce-scatter.27.cloned.1.call-update) | async-done | bytes 65552 | tf_op jit(solution)/shard_map/reduce_scatter | solution.py:337
  (408 shorter events, 237.6 us)
Async XLA Ops:
  7.2 118.6 %copy-start = (f32[256,2048]{1,0:T(8,128)S(1)}, f32[256,2048]{1,0:T(8,128)}, u32[]{:S(2)}) copy-start(f32[256,2048]{1,0:T(8,128)} %param.15) | copy-start | bytes 6291460
  7.2 122.2 %all-gather.30.cloned.1.call-start = ((), (), s32[]{:S(2)}) async-start(), calls=%async_computation.28 | async-start | bytes 1081344 | tf_op jit(solution)/shard_map/all_gather | solution.py:142
  7.9 121.5 %all-gather.32.cloned.1.call-start = ((), (), s32[]{:S(2)}) async-start(), calls=%async_computation.29 | async-start | bytes 1081344 | tf_op jit(solution)/shard_map/all_gather | solution.py:143
  8.7 197.6 %all-gather.20.cloned.1.call-start = ((), (), s32[]{:S(2)}) async-start(), calls=%async_computation.12 | async-start | bytes 5242880 | tf_op jit(solution)/shard_map/all_gather | solution.py:150
  91.7 35.3 %copy-start.19 = (f32[256]{0:T(256)}, f32[256]{0:T(256)S(1)}, u32[]{:S(2)}) copy-start(f32[256]{0:T(256)S(1)} %get-tuple-element.350) | copy-start | bytes 3076
  125.2 3.6 copy-start.22
  127.0 107.3 %all-gather.28.cloned.1.call-start = ((), (), s32[]{:S(2)}) async-start(), calls=%async_computation.27 | async-start | bytes 2359296 | tf_op jit(solution)/shard_map/all_gather | solution.py:135
  127.6 162.6 %all-gather.34.cloned.1.call-start = ((), (), s32[]{:S(2)}) async-start(), calls=%async_computation.30 | async-start | bytes 2359296 | tf_op jit(solution)/shard_map/all_gather | solution.py:136
  128.2 314.3 %reduce-scatter.15.cloned.1.call-start = ((), (), s32[]{:S(2)}) async-start(), calls=%async_computation.13 | async-start | bytes 10485760 | tf_op jit(solution)/shard_map/reduce_scatter | solution.py:154
  129.3 110.2 %copy-start.7 = (f32[1024,32]{0,1:T(8,128)}, f32[1024,32]{0,1:T(8,128)S(1)}, u32[]{:S(2)}) copy-start(f32[1024,32]{0,1:T(8,128)S(1)} %get-tuple-element.348) | copy-start | bytes 393220
  131.0 80.3 %copy-start.5 = (bf16[1,2048,64]{2,1,0:T(8,128)(2,1)}, bf16[1,2048,64]{2,1,0:T(8,128)(2,1)S(1)}, u32[]{:S(2)}) copy-start(bf16[1,2048,64]{2,1,0:T(8,128)(2,1)S(1)} %get-tuple-element.354) | copy-start | bytes 786436
  131.0 80.3 %copy-start.6 = (bf16[1,2048,64]{2,1,0:T(8,128)(2,1)}, bf16[1,2048,64]{2,1,0:T(8,128)(2,1)S(1)}, u32[]{:S(2)}) copy-start(bf16[1,2048,64]{2,1,0:T(8,128)(2,1)S(1)} %get-tuple-element.353) | copy-start | bytes 786436
  206.3 5.0 copy-start.4
  212.7 26.9 %copy-start.10 = (bf16[1024,64]{0,1:T(8,128)(2,1)}, bf16[1024,64]{0,1:T(8,128)(2,1)S(1)}, u32[]{:S(2)}) copy-start(bf16[1024,64]{0,1:T(8,128)(2,1)S(1)} %convolution_convert_fusion.6) | copy-start | bytes 393220
  297.8 228.3 %all-gather.24.cloned.1.call-start = ((), (), s32[]{:S(2)}) async-start(), calls=%async_computation.16 | async-start | bytes 5242880 | tf_op jit(solution)/shard_map/all_gather | solution.py:150
  300.5 270.2 %all-gather.40.cloned.1.call-start = ((), (), s32[]{:S(2)}) async-start(), calls=%async_computation.33 | async-start | bytes 6488064 | tf_op jit(solution)/shard_map/all_gather | solution.py:139
  301.3 314.5 %all-gather.38.cloned.1.call-start = ((), (), s32[]{:S(2)}) async-start(), calls=%async_computation.32 | async-start | bytes 6488064 | tf_op jit(solution)/shard_map/all_gather | solution.py:138
  302.0 396.5 %all-gather.22.cloned.1.call-start = ((), (), s32[]{:S(2)}) async-start(), calls=%async_computation.14 | async-start | bytes 5242880 | tf_op jit(solution)/shard_map/all_gather | solution.py:150
  447.0 295.2 %all-gather.36.cloned.1.call-start = ((), (), s32[]{:S(2)}) async-start(), calls=%async_computation.31 | async-start | bytes 6488064 | tf_op jit(solution)/shard_map/all_gather | solution.py:137
  447.7 475.3 %reduce-scatter.19.cloned.1.call-start = ((), (), s32[]{:S(2)}) async-start(), calls=%async_computation.17 | async-start | bytes 10485760 | tf_op jit(solution)/shard_map/reduce_scatter | solution.py:154
  742.2 16.1 copy-start.23
  758.2 9.0 copy-start.28
  758.2 9.0 copy-start.27
  758.2 9.0 copy-start.24
  778.3 292.4 %reduce-scatter.17.cloned.1.call-start = ((), (), s32[]{:S(2)}) async-start(), calls=%async_computation.15 | async-start | bytes 10485760 | tf_op jit(solution)/shard_map/reduce_scatter | solution.py:154
  790.4 132.7 %copy-start.3 = (f32[256,2048]{1,0:T(8,128)S(1)}, f32[256,2048]{1,0:T(8,128)}, u32[]{:S(2)}) copy-start(f32[256,2048]{1,0:T(8,128)} %copy-done.2) | copy-start | bytes 6291460
  790.4 367.7 %all-gather.26.cloned.1.call-start = ((), (), s32[]{:S(2)}) async-start(), calls=%async_computation.18 | async-start | bytes 5242880 | tf_op jit(solution)/shard_map/all_gather | solution.py:150
  1070.6 10.0 copy-start.9
  1076.6 4.7 copy-start.11
  1076.6 417.9 %reduce-scatter.21.cloned.1.call-start = ((), (), s32[]{:S(2)}) async-start(), calls=%async_computation.19 | async-start | bytes 10485760 | tf_op jit(solution)/shard_map/reduce_scatter | solution.py:154
  1334.5 1.8 copy-start.8
  1340.7 2.3 copy-start.25
  1343.0 2.4 copy-start.14
  1343.1 2.4 copy-start.15
  1351.3 206.3 %reduce-scatter.33.cloned.1.call-start = ((), (), s32[]{:S(2)}) async-start(), calls=%async_computation.25 | async-start | bytes 6488064 | tf_op jit(solution)/shard_map/reduce_scatter | solution.py:326
  1362.5 257.3 %reduce-scatter.31.cloned.1.call-start = ((), (), s32[]{:S(2)}) async-start(), calls=%async_computation.24 | async-start | bytes 6488064 | tf_op jit(solution)/shard_map/reduce_scatter | solution.py:323
  1373.6 308.4 %reduce-scatter.35.cloned.1.call-start = ((), (), s32[]{:S(2)}) async-start(), calls=%async_computation.26 | async-start | bytes 6488064 | tf_op jit(solution)/shard_map/reduce_scatter | solution.py:329
  1384.2 6.4 copy-start.26
  1384.2 342.3 %reduce-scatter.23.cloned.1.call-start = ((), (), s32[]{:S(2)}) async-start(), calls=%async_computation.20 | async-start | bytes 2359296 | tf_op jit(solution)/shard_map/reduce_scatter | solution.py:317
  1390.3 104.2 %copy-start.17 = (f32[2048]{0:T(1024)S(1)}, f32[2048]{0:T(1024)}, u32[]{:S(2)}) copy-start(f32[2048]{0:T(1024)} %copy-done.16) | copy-start | bytes 24580
  1390.3 104.2 %copy-start.20 = (f32[256]{0:T(256)S(1)}, f32[256]{0:T(256)}, u32[]{:S(2)}) copy-start(f32[256]{0:T(256)} %copy-done.19) | copy-start | bytes 3076
  1390.3 380.5 %reduce-scatter.29.cloned.1.call-start = ((), (), s32[]{:S(2)}) async-start(), calls=%async_computation.23 | async-start | bytes 2359296 | tf_op jit(solution)/shard_map/reduce_scatter | solution.py:320
  1396.5 98.0 %copy-start.1 = (f32[256,2048]{1,0:T(8,128)S(1)}, f32[256,2048]{1,0:T(8,128)}, u32[]{:S(2)}) copy-start(f32[256,2048]{1,0:T(8,128)} %param.15) | copy-start | bytes 6291460
  1396.5 100.2 %copy-start.18 = (f32[2048]{0:T(1024)S(1)}, f32[2048]{0:T(1024)}, u32[]{:S(2)}) copy-start(f32[2048]{0:T(1024)} %get-tuple-element.287) | copy-start | bytes 24580
  1396.5 513.6 %reduce-scatter.37.cloned.1.call-start = ((), (), s32[]{:S(2)}) async-start(), calls=%async_computation.34 | async-start | bytes 1081344
  1498.1 551.6 %reduce-scatter.25.cloned.1.call-start = ((), (), s32[]{:S(2)}) async-start(), calls=%async_computation.21 | async-start | bytes 2162688 | tf_op jit(solution)/shard_map/reduce_scatter | solution.py:336
  1512.4 677.5 %reduce-scatter.27.cloned.1.call-start = ((), (), s32[]{:S(2)}) async-start(), calls=%async_computation.22 | async-start | bytes 2162688 | tf_op jit(solution)/shard_map/reduce_scatter | solution.py:337
  1559.8 212.7 %copy-start.21 = (f32[256]{0:T(256)S(1)}, f32[256]{0:T(256)}, u32[]{:S(2)}) copy-start(f32[256]{0:T(256)} %get-tuple-element.349) | copy-start | bytes 3076
  (4 other events, 4.1 us)
Sparse Core Ops, SparseCore 0:
  11.0 57.2 all-gather.29
  71.3 53.0 all-gather.31
  127.1 79.0 all-gather.19
  208.0 26.2 all-gather.27
  236.0 28.0 all-gather.33
  297.9 144.6 reduce-scatter.14
  444.7 81.3 all-gather.23
  527.9 42.7 all-gather.39
  572.6 43.1 all-gather.37
  617.8 80.7 all-gather.21
  700.5 41.6 all-gather.35
  778.4 144.6 reduce-scatter.18
  925.4 145.2 reduce-scatter.16
  1076.7 81.3 all-gather.25
  1351.4 143.0 reduce-scatter.20
  1497.8 59.6 reduce-scatter.32
  1560.8 58.9 reduce-scatter.30
  1623.2 58.8 reduce-scatter.34
  1685.3 41.1 reduce-scatter.22
  1729.6 41.1 reduce-scatter.28
  1773.0 137.0 reduce-scatter.36
  1913.0 136.6 reduce-scatter.24
  2052.5 137.3 reduce-scatter.26
where the time goes:
time: 2210 us; the launch traced here: 2200 us
  waiting for transfers between devices  1610 us (73%)
  local copies, waits for them, and re-layouts  207 us (9%)
  matrix products  204 us (9%)
  blocking collectives  79.8 us (4%)
  other arithmetic  78.1 us (4%)
    reduce_scatter x4, waiting for transfers between devices, sum_rows(): lax.psum_scatter(term(jnp.int32(0), rows_dev * lax.axis_size('tensor')),...  516 us
    all_gather x4, waiting for transfers between devices, gather_rows(): return lax.all_gather(row_vals, 'tensor', axis=0, tiled=True)  313 us
    reduce_scatter x1, waiting for transfers between devices, on_device(): lax.psum_scatter(grad_value, ('dp', 'tensor'), scatter_dimension=0, tiled...  140 us
    unnamed x24, waiting for transfers between devices  138 us
    reduce_scatter x1, waiting for transfers between devices, on_device(): lax.psum_scatter(grad_key, ('dp', 'tensor'), scatter_dimension=0, tiled=T...  138 us
    dynamic_update_slice x32, local copies, waits for them, and re-layouts, on_device(): lax.map(one_backward, (by_sequence(query_all), by_sequence(key_all), by_s...  135 us
    all_gather x1, blocking collectives, fetch_weights(): lax.all_gather(norm_gains[layer_index], ('dp', 'tensor'), axis=1, tiled=T...  79.8 us
    reduce_scatter x1, waiting for transfers between devices, on_device(): lax.psum_scatter(grad_gate.astype(jnp.bfloat16), 'dp', scatter_dimension=...  60 us
  transfers between devices with their start and end apart: 23, of which 20 were waited for; matrix products, arithmetic and copies ran while one was open for 11% of the time, Pallas kernels for 0%

commit v1 on v0

--- a/solution.py
+++ b/solution.py
@@ -10,6 +10,27 @@
 SEQ = 128
 NORM_EPS = 1e-05
 NEG_BIG = -1e30
+
+
+def collect(value, axis, dim):
+    devices, index, extent = (lax.axis_size(axis), lax.axis_index(axis), value.shape[dim])
+    right = [(i, (i + 1) % devices) for i in range(devices)]
+    left = [(i, (i - 1) % devices) for i in range(devices)]
+    filled = jnp.zeros((*value.shape[:dim], devices * extent, *value.shape[dim + 1 :]), value.dtype)
+    filled = lax.dynamic_update_slice_in_dim(filled, value, index * extent, axis=dim)
+    from_left = from_right = value
+    halfway = devices // 2
+    for step in range(1, halfway + 1):
+        from_left = lax.ppermute(from_left, axis, right)
+        filled = lax.dynamic_update_slice_in_dim(
+            filled, from_left, (index - step) % devices * extent, axis=dim
+        )
+        if step < devices - halfway:
+            from_right = lax.ppermute(from_right, axis, left)
+            filled = lax.dynamic_update_slice_in_dim(
+                filled, from_right, (index + step) % devices * extent, axis=dim
+            )
+    return filled
 
 
 def rms_normed(row_vals, gain_vec):
@@ -147,7 +168,7 @@
 
 
 def gather_rows(row_vals):
-    return lax.all_gather(row_vals, "tensor", axis=0, tiled=True)
+    return collect(row_vals, "tensor", 0)
 
 
 def sum_rows(term, rows_dev):

time: 2210 us -> 2080 us (0.941)
  waiting for transfers between devices: 1610 us -> 1360 us
  starting transfers between devices: 2.19 us -> 85.5 us
  local copies, waits for them, and re-layouts: 207 us -> 242 us
    all_gather x4 -> x0, waiting for transfers between devices: 313 us -> none  [gather_rows(): return lax.all_gather(row_vals, 'tensor', axis=0, tiled=True)]
    ppermute x0 -> x12, waiting for transfers between devices: none -> 166 us  [the longest x8 150 us: collect(): from_left = lax.ppermute(from_left, axis, right)]
    ppermute x0 -> x12, starting transfers between devices: none -> 84.5 us  [the longest x8 70.2 us: collect(): from_left = lax.ppermute(from_left, axis, right)]
    all_gather x1, waiting for transfers between devices: 44.7 us -> 0.01 us  [fetch_weights(): lax.all_gather(w_down[layer_index], 'dp', axis=1, tiled=True)]
    dynamic_update_slice x0 -> x12, local copies, waits for them, and re-layouts: none -> 24.3 us  [the longest x8 14.9 us: collect(): lax.dynamic_update_slice_in_dim(filled, from_left, (index - step) % devic...]
    unnamed x24 -> x20, waiting for transfers between devices: 138 us -> 137 us
  transfers between devices with their start and end apart: 23 -> 31, of which waited for: 20 -> 22; matrix products, arithmetic and copies ran while one was open for 11% -> 13% of each run, Pallas kernels for 0% -> 0%
where the time goes in v1:
time: 2080 us; the launch traced here: 2070 us
  waiting for transfers between devices  1360 us (65%)
  local copies, waits for them, and re-layouts  242 us (12%)
  matrix products  205 us (10%)
  starting transfers between devices  85.5 us (4%)
  blocking collectives  79.8 us (4%)
  other arithmetic  76 us (4%)
    reduce_scatter x4, waiting for transfers between devices, sum_rows(): lax.psum_scatter(term(jnp.int32(0), rows_dev * lax.axis_size('tensor')),...  499 us
    ppermute x8, waiting for transfers between devices, collect(): from_left = lax.ppermute(from_left, axis, right)  150 us
    reduce_scatter x1, waiting for transfers between devices, on_device(): lax.psum_scatter(grad_key, ('dp', 'tensor'), scatter_dimension=0, tiled=T...  140 us
    reduce_scatter x1, waiting for transfers between devices, on_device(): lax.psum_scatter(grad_value, ('dp', 'tensor'), scatter_dimension=0, tiled...  138 us
    unnamed x20, waiting for transfers between devices  137 us
    dynamic_update_slice x32, local copies, waits for them, and re-layouts, on_device(): lax.map(one_backward, (by_sequence(query_all), by_sequence(key_all), by_s...  135 us
    all_gather x1, blocking collectives, fetch_weights(): lax.all_gather(norm_gains[layer_index], ('dp', 'tensor'), axis=1, tiled=T...  79.8 us
    ppermute x8, starting transfers between devices, collect(): from_left = lax.ppermute(from_left, axis, right)  70.2 us
  transfers between devices with their start and end apart: 31, of which 22 were waited for; matrix products, arithmetic and copies ran while one was open for 13% of the time, Pallas kernels for 0%

profile of v1, /device:TPU:0, one launch (start us, length us, event | category | flops | bytes accessed | tf_op | source)
XLA Modules:
  0.0 2069.1 jit_solution(12077392701916140325)
XLA Ops:
  10.2 79.8 %all-gather = bf16[1,2,2048]{1,0,2:T(2,128)(2,1)S(1)} all-gather(bf16[1,2,64]{1,0,2:T(2,128)(2,1)S(1)} %copy.87), channel_id=2, replica_groups=mesh['dp'=8,'tensor'=4] {'dp','tensor'}, dimensions={2}, use_global_device_ids=true | all-gather | bytes 8448 | tf_op jit(solution)/shard_map/all_gather | solution.py:165
  92.6 33.9 %fusion.68 = (f32[2048]{0:T(1024)S(1)}, f32[2048]{0:T(1024)S(1)}) fusion(bf16[1,2,2048]{1,0,2:T(2,128)(2,1)S(1)} %all-gather), kind=kLoop, calls=%fused_computation.104 | loop fusion | flops 4096 | bytes 24576 | tf_op jit(solution)/shard_map/mul | solution.py:38
  134.4 23.9 %collective-permute-done = bf16[256,2048]{1,0:T(8,128)(2,1)} collective-permute-done((bf16[256,2048]{1,0:T(8,128)(2,1)S(1)}, bf16[256,2048]{1,0:T(8,128)(2,1)}, u32[]{:S(2)}, u32[]{:S(2)}) %collective-permute-start) | collective-permute-done | bytes 1048608 | tf_op jit(solution)/shard_map/ppermute | solution.py:24
  161.2 16.0 collective-permute-done.1
  181.1 16.0 collective-permute-done.2
  214.7 49.7 %while.30 = (s32[]{:T(128)}, bf16[8,128,512]{2,1,0:T(8,128)(2,1)}, f32[8,1024]{1,0:T(8,128)}, bf16[8,128,512]{1,2,0:T(8,128)(2,1)S(1)}, bf16[8,128,64]{1,0,2:T(8...) while((s32[]{:T(128)}, bf16[8,128,512]{2,1,0:T(8,128)(2,1)}, f32[8,1024]{1,0:T(8,128)}, ...), condition=%wide.region_4.5_spmd, body=%wide.region_1.4_spmd.sunk | while | flops 34804736 | bytes 3300449 | solution.py:227
  282.4 46.8 %collective-permute-done.6 = bf16[256,2048]{1,0:T(8,128)(2,1)} collective-permute-done((bf16[256,2048]{1,0:T(8,128)(2,1)}, bf16[256,2048]{1,0:T(8,128)(2,1)}, u32[]{:S(2)}, u32[]{:S(2)}) %collective-permute-start.6) | collective-permute-done | bytes 1048608 | tf_op jit(solution)/shard_map/ppermute | solution.py:24
  329.2 27.0 %collective-permute-start.8 = (bf16[256,2048]{1,0:T(8,128)(2,1)}, bf16[256,2048]{1,0:T(8,128)(2,1)}, u32[]{:S(2)}, u32[]{:S(2)}) collective-permute-start(bf16[256,2048]{1,0:T(8,128)(2,1)} %collective-permute-done.6), channel_id=1, source_target_pairs={{0,1},{1,2},{2,3},{3,0},{4,5},{5,6},{6,7},{7,4},{8,9},{9,10},{10,1... | collective-permute-start | bytes 3145736 | tf_op jit(solution)/shard_map/ppermute | solution.py:24
  356.1 122.7 %reduce-scatter.15.cloned.1.call-done = f32[256,2048]{1,0:T(8,128)} async-done(((f32[1024,2048]{1,0:T(8,128)}), f32[256,2048]{1,0:T(8,128)}) %reduce-scatter.15.cloned.1.call-update) | async-done | bytes 2097168 | tf_op jit(solution)/shard_map/reduce_scatter | solution.py:175
  495.7 16.9 collective-permute-done.3
  512.6 20.6 collective-permute-start.5
  533.2 11.8 fusion.32
  548.5 8.4 collective-permute-done.5
  559.1 14.1 all-gather.26.cloned.1.call-done
  573.2 11.7 fusion.38
  584.9 33.4 %all-gather.24.cloned.1.call-done = bf16[1,2048,1408]{2,1,0:T(8,128)(2,1)} async-done(((bf16[1,256,1408]{2,1,0:T(8,128)(2,1)}), bf16[1,2048,1408]{2,1,0:T(8,128)(2,1)}) %all-gather.24.cloned.1.call-update) | async-done | bytes 5767184 | tf_op jit(solution)/shard_map/all_gather | solution.py:158
  618.3 16.1 multiply_convert_fusion.2
  634.4 9.0 fusion.36
  643.4 11.2 fusion.48
  654.7 11.6 fusion.34
  666.4 133.0 %reduce-scatter.19.cloned.1.call-done = f32[256,2048]{1,0:T(8,128)} async-done(((f32[1024,2048]{1,0:T(8,128)}), f32[256,2048]{1,0:T(8,128)}) %reduce-scatter.19.cloned.1.call-update) | async-done | bytes 2097168 | tf_op jit(solution)/shard_map/reduce_scatter | solution.py:175
  799.4 147.5 %reduce-scatter.17.cloned.1.call-done = f32[256,2048]{1,0:T(8,128)} async-done(((f32[1024,2048]{1,0:T(8,128)}), f32[256,2048]{1,0:T(8,128)}) %reduce-scatter.17.cloned.1.call-update) | async-done | bytes 2097168 | tf_op jit(solution)/shard_map/reduce_scatter | solution.py:175
  962.0 24.3 %collective-permute-done.9 = bf16[256,2048]{1,0:T(8,128)(2,1)S(1)} collective-permute-done((bf16[256,2048]{1,0:T(8,128)(2,1)}, bf16[256,2048]{1,0:T(8,128)(2,1)S(1)}, u32[]{:S(2)}, u32[]{:S(2)}) %collective-permute-start.9) | collective-permute-done | bytes 1048608 | tf_op jit(solution)/shard_map/ppermute | solution.py:24
  986.2 21.6 %collective-permute-start.11 = (bf16[256,2048]{1,0:T(8,128)(2,1)S(1)}, bf16[256,2048]{1,0:T(8,128)(2,1)S(1)}, u32[]{:S(2)}, u32[]{:S(2)}) collective-permute-start(bf16[256,2048]{1,0:T(8,128)(2,1)S(1)} %collective-permute-done.9), channel_id=1, source_target_pairs={{0,1},{1,2},{2,3},{3,0},{4,5},{5,6},{6,7},{7,4},{8,9},{9,10},{10,1... | collective-permute-start | bytes 3145736 | tf_op jit(solution)/shard_map/ppermute | solution.py:24
  1015.9 13.8 collective-permute-done.11
  1035.3 171.4 %while.31 = (s32[]{:T(128)}, f32[8,128,512]{1,0,2:T(8,128)}, f32[8,128,512]{1,0,2:T(8,128)}, bf16[8,128,512]{2,1,0:T(8,128)(2,1)}, bf16[8,128,512]{1,2,0:T(8,128...) while((s32[]{:T(128)}, f32[8,128,512]{1,0,2:T(8,128)}, ...), condition=%wide.region_12.13_spmd, body=%wide.region_10.12_spmd.sunk | while | flops 85464064 | bytes 7626373 | solution.py:302
  1060.5 8.0 dynamic_update_slice.132
  1069.4 8.0 dynamic_update_slice.131
  1081.8 8.0 dynamic_update_slice.132
  1090.8 8.0 dynamic_update_slice.131
  1103.2 8.0 dynamic_update_slice.132
  1112.2 8.0 dynamic_update_slice.131
  1124.6 8.0 dynamic_update_slice.132
  1133.5 8.0 dynamic_update_slice.131
  1167.3 8.0 dynamic_update_slice.132
  1176.3 8.0 dynamic_update_slice.131
  1223.3 11.1 convolution_convert_fusion.2
  1234.5 11.0 convolution_convert_fusion.3
  1245.6 10.5 convolution_convert_fusion.1
  1270.9 96.2 %reduce-scatter.21.cloned.1.call-done = f32[256,2048]{1,0:T(8,128)} async-done(((f32[1024,2048]{1,0:T(8,128)}), f32[256,2048]{1,0:T(8,128)}) %reduce-scatter.21.cloned.1.call-update) | async-done | bytes 2097168 | tf_op jit(solution)/shard_map/reduce_scatter | solution.py:175
  1399.7 30.3 %reduce-scatter.33.cloned.1.call-done = bf16[256,1408]{1,0:T(8,128)(2,1)} async-done(((bf16[2048,1408]{1,0:T(8,128)(2,1)}), bf16[256,1408]{1,0:T(8,128)(2,1)}) %reduce-scatter.33.cloned.1.call-update) | async-done | bytes 720912 | tf_op jit(solution)/shard_map/reduce_scatter | solution.py:347
  1432.4 60.2 %reduce-scatter.31.cloned.1.call-done = bf16[256,1408]{1,0:T(8,128)(2,1)} async-done(((bf16[2048,1408]{1,0:T(8,128)(2,1)}), bf16[256,1408]{1,0:T(8,128)(2,1)}) %reduce-scatter.31.cloned.1.call-update) | async-done | bytes 720912 | tf_op jit(solution)/shard_map/reduce_scatter | solution.py:344
  1494.9 59.9 %reduce-scatter.35.cloned.1.call-done = bf16[1408,256]{1,0:T(8,128)(2,1)} async-done(((bf16[1408,2048]{1,0:T(8,128)(2,1)}), bf16[1408,256]{1,0:T(8,128)(2,1)}) %reduce-scatter.35.cloned.1.call-update) | async-done | bytes 720912 | tf_op jit(solution)/shard_map/reduce_scatter | solution.py:350
  1557.1 42.0 %reduce-scatter.29.cloned.1.call-done = bf16[512,256]{1,0:T(8,128)(2,1)} async-done(((bf16[512,2048]{1,0:T(8,128)(2,1)}), bf16[512,256]{1,0:T(8,128)(2,1)}) %reduce-scatter.29.cloned.1.call-update) | async-done | bytes 262160 | tf_op jit(solution)/shard_map/reduce_scatter | solution.py:341
  1600.8 42.5 %reduce-scatter.23.cloned.1.call-done = bf16[256,512]{1,0:T(8,128)(2,1)} async-done(((bf16[2048,512]{1,0:T(8,128)(2,1)}), bf16[256,512]{1,0:T(8,128)(2,1)}) %reduce-scatter.23.cloned.1.call-update) | async-done | bytes 262160 | tf_op jit(solution)/shard_map/reduce_scatter | solution.py:338
  1649.3 133.2 %reduce-scatter.37.cloned.1.call-done = f32[64,2]{1,0:T(8,128)} async-done(((f32[2048,2]{1,0:T(8,128)}), f32[64,2]{1,0:T(8,128)}) %reduce-scatter.37.cloned.1.call-update) | async-done | bytes 528
  1783.8 138.2 %reduce-scatter.27.cloned.1.call-done = f32[64,256]{1,0:T(8,128)} async-done(((f32[2048,256]{1,0:T(8,128)}), f32[64,256]{1,0:T(8,128)}) %reduce-scatter.27.cloned.1.call-update) | async-done | bytes 65552 | tf_op jit(solution)/shard_map/reduce_scatter | solution.py:358
  1922.0 140.3 %reduce-scatter.25.cloned.1.call-done = f32[64,256]{1,0:T(8,128)} async-done(((f32[2048,256]{1,0:T(8,128)}), f32[64,256]{1,0:T(8,128)}) %reduce-scatter.25.cloned.1.call-update) | async-done | bytes 65552 | tf_op jit(solution)/shard_map/reduce_scatter | solution.py:357
  (450 shorter events, 325.9 us)
Async XLA Ops:
  7.2 172.3 %all-gather.18.cloned.1.call-start = ((), (), s32[]{:S(2)}) async-start(), calls=%async_computation.24 | async-start | bytes 1081344 | tf_op jit(solution)/shard_map/all_gather | solution.py:163
  7.9 171.6 %all-gather.20.cloned.1.call-start = ((), (), s32[]{:S(2)}) async-start(), calls=%async_computation.25 | async-start | bytes 1081344 | tf_op jit(solution)/shard_map/all_gather | solution.py:164
  8.7 199.9 %all-gather.16.cloned.1.call-start = ((), (), s32[]{:S(2)}) async-start(), calls=%async_computation.23 | async-start | bytes 2359296 | tf_op jit(solution)/shard_map/all_gather | solution.py:156
  9.4 255.0 %all-gather.22.cloned.1.call-start = ((), (), s32[]{:S(2)}) async-start(), calls=%async_computation.26 | async-start | bytes 2359296 | tf_op jit(solution)/shard_map/all_gather | solution.py:157
  90.1 39.0 %copy-start = (f32[256,2048]{1,0:T(8,128)S(1)}, f32[256,2048]{1,0:T(8,128)}, u32[]{:S(2)}) copy-start(f32[256,2048]{1,0:T(8,128)} %param.15) | copy-start | bytes 6291460
  92.6 37.7 %copy-start.25 = (f32[256]{0:T(256)}, f32[256]{0:T(256)S(1)}, u32[]{:S(2)}) copy-start(f32[256]{0:T(256)S(1)} %get-tuple-element.357) | copy-start | bytes 3076
  130.3 27.9 %collective-permute-start = (bf16[256,2048]{1,0:T(8,128)(2,1)S(1)}, bf16[256,2048]{1,0:T(8,128)(2,1)}, u32[]{:S(2)}, u32[]{:S(2)}) collective-permute-start(bf16[256,2048]{1,0:T(8,128)(2,1)S(1)} %get-tuple-element.331), channel_id=1, source_target_pairs={{0,1},{1,2},{2,3},{3,0},{4,5},{5,6},{6,7},{7,4},{8,9},{9,10},{10,1... | collective-permute-start | bytes 3145736 | tf_op jit(solution)/shard_map/ppermute | solution.py:24
  130.3 46.8 %collective-permute-start.1 = (bf16[256,2048]{1,0:T(8,128)(2,1)S(1)}, bf16[256,2048]{1,0:T(8,128)(2,1)}, u32[]{:S(2)}, u32[]{:S(2)}) collective-permute-start(bf16[256,2048]{1,0:T(8,128)(2,1)S(1)} %get-tuple-element.331), channel_id=1, source_target_pairs={{0,3},{1,0},{2,1},{3,2},{4,7},{5,4},{6,5},{7,6},{8,11},{9,8},{10,9... | collective-permute-start | bytes 3145736 | tf_op jit(solution)/shard_map/ppermute | solution.py:29
  134.2 344.7 %reduce-scatter.15.cloned.1.call-start = ((), (), s32[]{:S(2)}) async-start(), calls=%async_computation.12 | async-start | bytes 10485760 | tf_op jit(solution)/shard_map/reduce_scatter | solution.py:175
  158.3 38.8 %collective-permute-start.2 = (bf16[256,2048]{1,0:T(8,128)(2,1)}, bf16[256,2048]{1,0:T(8,128)(2,1)}, u32[]{:S(2)}, u32[]{:S(2)}) collective-permute-start(bf16[256,2048]{1,0:T(8,128)(2,1)} %collective-permute-done), channel_id=1, source_target_pairs={{0,1},{1,2},{2,3},{3,0},{4,5},{5,6},{6,7},{7,4},{8,9},{9,10},{10,1... | collective-permute-start | bytes 3145736 | tf_op jit(solution)/shard_map/ppermute | solution.py:24
  158.8 55.0 %copy-start.10 = (f32[1024,32]{0,1:T(8,128)}, f32[1024,32]{0,1:T(8,128)S(1)}, u32[]{:S(2)}) copy-start(f32[1024,32]{0,1:T(8,128)S(1)} %get-tuple-element.355) | copy-start | bytes 393220
  181.0 26.8 %copy-start.7 = (bf16[1,2048,64]{2,1,0:T(8,128)(2,1)}, bf16[1,2048,64]{2,1,0:T(8,128)(2,1)S(1)}, u32[]{:S(2)}) copy-start(bf16[1,2048,64]{2,1,0:T(8,128)(2,1)S(1)} %get-tuple-element.361) | copy-start | bytes 786436
  181.0 26.8 %copy-start.8 = (bf16[1,2048,64]{2,1,0:T(8,128)(2,1)}, bf16[1,2048,64]{2,1,0:T(8,128)(2,1)S(1)}, u32[]{:S(2)}) copy-start(bf16[1,2048,64]{2,1,0:T(8,128)(2,1)S(1)} %get-tuple-element.360) | copy-start | bytes 786436
  272.0 261.2 %all-gather.28.cloned.1.call-start = ((), (), s32[]{:S(2)}) async-start(), calls=%async_computation.29 | async-start | bytes 6488064 | tf_op jit(solution)/shard_map/all_gather | solution.py:160
  272.6 300.6 %all-gather.26.cloned.1.call-start = ((), (), s32[]{:S(2)}) async-start(), calls=%async_computation.28 | async-start | bytes 6488064 | tf_op jit(solution)/shard_map/all_gather | solution.py:159
  273.3 345.0 %all-gather.24.cloned.1.call-start = ((), (), s32[]{:S(2)}) async-start(), calls=%async_computation.27 | async-start | bytes 6488064 | tf_op jit(solution)/shard_map/all_gather | solution.py:158
  274.1 525.3 %reduce-scatter.19.cloned.1.call-start = ((), (), s32[]{:S(2)}) async-start(), calls=%async_computation.14 | async-start | bytes 10485760 | tf_op jit(solution)/shard_map/reduce_scatter | solution.py:175
  278.5 50.6 %collective-permute-start.6 = (bf16[256,2048]{1,0:T(8,128)(2,1)}, bf16[256,2048]{1,0:T(8,128)(2,1)}, u32[]{:S(2)}, u32[]{:S(2)}) collective-permute-start(bf16[256,2048]{1,0:T(8,128)(2,1)} %get-tuple-element.325), channel_id=1, source_target_pairs={{0,1},{1,2},{2,3},{3,0},{4,5},{5,6},{6,7},{7,4},{8,9},{9,10},{10,1... | collective-permute-start | bytes 3145736 | tf_op jit(solution)/shard_map/ppermute | solution.py:24
  278.6 208.5 %collective-permute-start.7 = (bf16[256,2048]{1,0:T(8,128)(2,1)}, bf16[256,2048]{1,0:T(8,128)(2,1)}, u32[]{:S(2)}, u32[]{:S(2)}) collective-permute-start(bf16[256,2048]{1,0:T(8,128)(2,1)} %get-tuple-element.325), channel_id=1, source_target_pairs={{0,3},{1,0},{2,1},{3,2},{4,7},{5,4},{6,5},{7,6},{8,11},{9,8},{10,9... | collective-permute-start | bytes 3145736 | tf_op jit(solution)/shard_map/ppermute | solution.py:29
  329.2 160.3 %collective-permute-start.8 = (bf16[256,2048]{1,0:T(8,128)(2,1)}, bf16[256,2048]{1,0:T(8,128)(2,1)}, u32[]{:S(2)}, u32[]{:S(2)}) collective-permute-start(bf16[256,2048]{1,0:T(8,128)(2,1)} %collective-permute-done.6), channel_id=1, source_target_pairs={{0,1},{1,2},{2,3},{3,0},{4,5},{5,6},{6,7},{7,4},{8,9},{9,10},{10,1... | collective-permute-start | bytes 3145736 | tf_op jit(solution)/shard_map/ppermute | solution.py:24
  484.8 27.9 %collective-permute-start.3 = (bf16[256,2048]{1,0:T(8,128)(2,1)S(1)}, bf16[256,2048]{1,0:T(8,128)(2,1)S(1)}, u32[]{:S(2)}, u32[]{:S(2)}) collective-permute-start(bf16[256,2048]{1,0:T(8,128)(2,1)S(1)} %get-tuple-element.327), channel_id=1, source_target_pairs={{0,1},{1,2},{2,3},{3,0},{4,5},{5,6},{6,7},{7,4},{8,9},{9,10},{10,1... | collective-permute-start | bytes 3145736 | tf_op jit(solution)/shard_map/ppermute | solution.py:24
  491.9 54.2 %collective-permute-start.4 = (bf16[256,2048]{1,0:T(8,128)(2,1)S(1)}, bf16[256,2048]{1,0:T(8,128)(2,1)}, u32[]{:S(2)}, u32[]{:S(2)}) collective-permute-start(bf16[256,2048]{1,0:T(8,128)(2,1)S(1)} %get-tuple-element.327), channel_id=1, source_target_pairs={{0,3},{1,0},{2,1},{3,2},{4,7},{5,4},{6,5},{7,6},{8,11},{9,8},{10,9... | collective-permute-start | bytes 3145736 | tf_op jit(solution)/shard_map/ppermute | solution.py:29
  512.6 44.2 %collective-permute-start.5 = (bf16[256,2048]{1,0:T(8,128)(2,1)S(1)}, bf16[256,2048]{1,0:T(8,128)(2,1)}, u32[]{:S(2)}, u32[]{:S(2)}) collective-permute-start(bf16[256,2048]{1,0:T(8,128)(2,1)S(1)} %collective-permute-done.3), channel_id=1, source_target_pairs={{0,1},{1,2},{2,3},{3,0},{4,5},{5,6},{6,7},{7,4},{8,9},{9,10},{10,1... | collective-permute-start | bytes 3145736 | tf_op jit(solution)/shard_map/ppermute | solution.py:24
  618.3 16.1 copy-start.29
  634.4 9.0 copy-start.34
  654.6 292.2 %reduce-scatter.17.cloned.1.call-start = ((), (), s32[]{:S(2)}) async-start(), calls=%async_computation.13 | async-start | bytes 10485760 | tf_op jit(solution)/shard_map/reduce_scatter | solution.py:175
  666.3 280.5 %copy-start.3 = (f32[256,2048]{1,0:T(8,128)S(1)}, f32[256,2048]{1,0:T(8,128)}, u32[]{:S(2)}) copy-start(f32[256,2048]{1,0:T(8,128)} %copy-done.2) | copy-start | bytes 6291460
  666.3 700.8 %reduce-scatter.21.cloned.1.call-start = ((), (), s32[]{:S(2)}) async-start(), calls=%async_computation.15 | async-start | bytes 10485760 | tf_op jit(solution)/shard_map/reduce_scatter | solution.py:175
  953.7 58.0 %copy-start.12 = (bf16[8,128,64]{1,0,2:T(8,128)(2,1)S(1)}, bf16[8,128,64]{1,0,2:T(8,128)(2,1)}, u32[]{:S(2)}) copy-start(bf16[8,128,64]{1,0,2:T(8,128)(2,1)} %get-tuple-element.579) | copy-start | bytes 393220
  953.7 58.7 %copy-start.14 = (bf16[1024,64]{0,1:T(8,128)(2,1)S(1)}, bf16[1024,64]{0,1:T(8,128)(2,1)}, u32[]{:S(2)}) copy-start(bf16[1024,64]{0,1:T(8,128)(2,1)} %copy-done.13) | copy-start | bytes 393220
  958.2 28.1 %collective-permute-start.9 = (bf16[256,2048]{1,0:T(8,128)(2,1)}, bf16[256,2048]{1,0:T(8,128)(2,1)S(1)}, u32[]{:S(2)}, u32[]{:S(2)}) collective-permute-start(bf16[256,2048]{1,0:T(8,128)(2,1)} %get-tuple-element.322), channel_id=1, source_target_pairs={{0,1},{1,2},{2,3},{3,0},{4,5},{5,6},{6,7},{7,4},{8,9},{9,10},{10,1... | collective-permute-start | bytes 3145736 | tf_op jit(solution)/shard_map/ppermute | solution.py:24
  959.2 54.3 %collective-permute-start.10 = (bf16[256,2048]{1,0:T(8,128)(2,1)}, bf16[256,2048]{1,0:T(8,128)(2,1)}, u32[]{:S(2)}, u32[]{:S(2)}) collective-permute-start(bf16[256,2048]{1,0:T(8,128)(2,1)} %get-tuple-element.322), channel_id=1, source_target_pairs={{0,3},{1,0},{2,1},{3,2},{4,7},{5,4},{6,5},{7,6},{8,11},{9,8},{10,9... | collective-permute-start | bytes 3145736 | tf_op jit(solution)/shard_map/ppermute | solution.py:29
  986.2 43.4 %collective-permute-start.11 = (bf16[256,2048]{1,0:T(8,128)(2,1)S(1)}, bf16[256,2048]{1,0:T(8,128)(2,1)S(1)}, u32[]{:S(2)}, u32[]{:S(2)}) collective-permute-start(bf16[256,2048]{1,0:T(8,128)(2,1)S(1)} %collective-permute-done.9), channel_id=1, source_target_pairs={{0,1},{1,2},{2,3},{3,0},{4,5},{5,6},{6,7},{7,4},{8,9},{9,10},{10,1... | collective-permute-start | bytes 3145736 | tf_op jit(solution)/shard_map/ppermute | solution.py:24
  1011.7 19.0 copy-start.32
  1223.2 206.8 %reduce-scatter.33.cloned.1.call-start = ((), (), s32[]{:S(2)}) async-start(), calls=%async_computation.21 | async-start | bytes 6488064 | tf_op jit(solution)/shard_map/reduce_scatter | solution.py:347
  1234.5 258.1 %reduce-scatter.31.cloned.1.call-start = ((), (), s32[]{:S(2)}) async-start(), calls=%async_computation.20 | async-start | bytes 6488064 | tf_op jit(solution)/shard_map/reduce_scatter | solution.py:344
  1245.5 309.2 %reduce-scatter.35.cloned.1.call-start = ((), (), s32[]{:S(2)}) async-start(), calls=%async_computation.22 | async-start | bytes 6488064 | tf_op jit(solution)/shard_map/reduce_scatter | solution.py:350
  1256.1 343.0 %reduce-scatter.29.cloned.1.call-start = ((), (), s32[]{:S(2)}) async-start(), calls=%async_computation.19 | async-start | bytes 2359296 | tf_op jit(solution)/shard_map/reduce_scatter | solution.py:341
  1263.3 380.1 %reduce-scatter.23.cloned.1.call-start = ((), (), s32[]{:S(2)}) async-start(), calls=%async_computation.16 | async-start | bytes 2359296 | tf_op jit(solution)/shard_map/reduce_scatter | solution.py:338
  1269.5 97.6 %copy-start.1 = (f32[256,2048]{1,0:T(8,128)S(1)}, f32[256,2048]{1,0:T(8,128)}, u32[]{:S(2)}) copy-start(f32[256,2048]{1,0:T(8,128)} %param.15) | copy-start | bytes 6291460
  1269.5 97.6 %copy-start.23 = (f32[2048]{0:T(1024)S(1)}, f32[2048]{0:T(1024)}, u32[]{:S(2)}) copy-start(f32[2048]{0:T(1024)} %copy-done.22) | copy-start | bytes 24580
  1269.5 97.6 %copy-start.26 = (f32[256]{0:T(256)S(1)}, f32[256]{0:T(256)}, u32[]{:S(2)}) copy-start(f32[256]{0:T(256)} %copy-done.25) | copy-start | bytes 3076
  1269.5 99.7 %copy-start.24 = (f32[2048]{0:T(1024)S(1)}, f32[2048]{0:T(1024)}, u32[]{:S(2)}) copy-start(f32[2048]{0:T(1024)} %get-tuple-element.287) | copy-start | bytes 24580
  1269.5 512.9 %reduce-scatter.37.cloned.1.call-start = ((), (), s32[]{:S(2)}) async-start(), calls=%async_computation.30 | async-start | bytes 1081344
  1270.9 99.9 %copy-start.18 = (bf16[512,1024]{1,0:T(8,128)(2,1)S(1)}, bf16[512,1024]{1,0:T(8,128)(2,1)}, u32[]{:S(2)}) copy-start(bf16[512,1024]{1,0:T(8,128)(2,1)} %copy.102) | copy-start | bytes 3145732
  1370.7 551.3 %reduce-scatter.27.cloned.1.call-start = ((), (), s32[]{:S(2)}) async-start(), calls=%async_computation.18 | async-start | bytes 2162688 | tf_op jit(solution)/shard_map/reduce_scatter | solution.py:358
  1385.1 677.2 %reduce-scatter.25.cloned.1.call-start = ((), (), s32[]{:S(2)}) async-start(), calls=%async_computation.17 | async-start | bytes 2162688 | tf_op jit(solution)/shard_map/reduce_scatter | solution.py:357
  1399.7 245.4 %copy-start.27 = (f32[256]{0:T(256)S(1)}, f32[256]{0:T(256)}, u32[]{:S(2)}) copy-start(f32[256]{0:T(256)} %get-tuple-element.356) | copy-start | bytes 3076
  (19 other events, 76.2 us)
Sparse Core Ops, SparseCore 0:
  11.0 56.7 all-gather.17
  70.8 53.2 all-gather.19
  125.9 26.7 all-gather.15
  154.4 28.0 all-gather.21
  272.1 206.6 reduce-scatter.14
  480.6 47.4 all-gather.27
  530.0 43.1 all-gather.25
  575.1 43.1 all-gather.23
  654.7 144.6 reduce-scatter.18
  801.6 145.2 reduce-scatter.16
  1223.4 143.6 reduce-scatter.20
  1370.4 59.6 reduce-scatter.32
  1433.5 59.0 reduce-scatter.30
  1495.9 58.8 reduce-scatter.34
  1557.9 41.1 reduce-scatter.28
  1602.2 41.1 reduce-scatter.22
  1645.5 136.9 reduce-scatter.36
  1785.1 136.8 reduce-scatter.26
  1924.8 137.4 reduce-scatter.24
